TPU v7x, 32 devices: a whole 2x2x4 slice. The times are simulated.
32 devices in a mesh: ov: 16 (over z, y, core), vec: 2 (over x).
Axes of the slice: x: 2, y: 2, z: 4, core: 2. Of those that a mesh axis runs over, the one named last changes fastest.
Arguments:
- chol_vectors: bfloat16 [196608, 4096], P('ov', 'vec'), may hold values from -3.5 to 3.5
- amplitudes: bfloat16 [196608, 256], P('ov'), may hold values from -0.013671875 to 0.013671875
- sigma_prior: bfloat16 [196608, 256], P(('ov', 'vec')), may hold values from -4 to 4
Outputs:
- sigma_cycle: bfloat16 [196608, 256], P(('ov', 'vec'))
All inputs are finite; a program needn't handle non-finite values.
Results may differ from a plain program's by a relative error of at most 0.0065.
Values may be sent and summed in bfloat16 or wider, within the bound.
A program may use at most 128 MiB of HBM per device.

v0:
```python
import functools

import jax
import jax.numpy as jnp
from jax import lax
from jax.experimental import pallas as pl
from jax.experimental.pallas import tpu as pltpu
from jax.sharding import PartitionSpec as P

MESH = pl.DeviceIdType.MESH
JT_ROWS = 16
CHUNK = 512
RING = 6
TILE_RING = 6


def halved(size, most):
    while size > most and size % 2 == 0:
        size //= 2
    return size


def divisor(size, choices):
    for choice in choices:
        if size % choice == 0:
            return choice
    return size


def kernel(
    plan, chol, amplitudes, prior, out,
    abuf, at, lbuf, acc, part, paired, halves, arrived, own, coup, weights, tiles, sbuf, rbuf, pbuf,
    a_sems, l_sems, t_sems, p_sem, swap_s, swap_r, scat_s, scat_r, gath_s, gath_r, on_s, on_r, x_s, x_r,
):
    n, groups, H, NC, NB, RB, VC, PV, JW, TR, NT = plan
    half = n // 2
    me = lax.axis_index("ov")
    vec = lax.axis_index("vec")
    side = lax.rem(me, 2)
    group = me // 2
    twin = me + 1 - 2 * side
    rows_out = TR * NT
    JT = JW // JT_ROWS
    VT = n // JT

    def mate(step):
        return 2 * lax.rem(group + step, half) + side

    def origin(step):
        return lax.rem(group + half - step, half)

    def l_copy(i):
        c, b = i // NB, lax.rem(i, NB)
        return pltpu.make_async_copy(
            chol.at[pl.ds(pl.multiple_of(b * RB, RB), RB), pl.ds(pl.multiple_of(c * VC, VC), VC)],
            lbuf.at[lax.rem(i, RING)],
            l_sems.at[lax.rem(i, RING)],
        )

    def a_copy(b):
        return pltpu.make_async_copy(
            amplitudes.at[pl.ds(pl.multiple_of(b * RB, RB), RB), :], abuf.at[b], a_sems.at[b]
        )

    total = NC * NB
    shares = NT * (groups - 1)
    jobs = H * (shares + NT)

    def job_row(q):
        final = q >= H * shares
        k = lax.rem(q, shares)
        t = jnp.where(final, lax.rem(q - H * shares, NT), k // (groups - 1))
        d = jnp.where(final, 0, lax.rem(k, groups - 1) + 1)
        return lax.rem(vec + d, groups) * rows_out + t * TR

    def t_copy(q):
        slot = lax.rem(q, TILE_RING)
        return pltpu.make_async_copy(
            chol.at[pl.ds(pl.multiple_of(job_row(q), TR), TR), :], tiles.at[slot], t_sems.at[slot]
        )

    barrier = pltpu.get_barrier_semaphore()
    pl.semaphore_signal(barrier, inc=1, device_id={"ov": twin}, device_id_type=MESH)

    @pl.loop(1, half)
    def _(step):
        pl.semaphore_signal(barrier, inc=1, device_id={"ov": mate(step)}, device_id_type=MESH)

    @pl.loop(1, groups)
    def _(d):
        pl.semaphore_signal(
            barrier, inc=1, device_id={"vec": lax.rem(vec + d, groups)}, device_id_type=MESH
        )

    for b in range(NB):
        a_copy(b).start()
        if b < min(RING, total):
            l_copy(jnp.int32(b)).start()
    for i in range(NB, min(RING, total)):
        l_copy(jnp.int32(i)).start()

    def compute(c, first, last):
        @pl.loop(first, last)
        def _(b):
            i = c * NB + b
            if c == 0:
                a_copy(b).wait()
                at[b] = abuf[b].T
            l_copy(i).wait()
            acc[...] += jnp.dot(at[b], lbuf[lax.rem(i, RING)], preferred_element_type=jnp.float32)

            @pl.when(i + RING < total)
            def _():
                l_copy(i + RING).start()

    def store_part(c):
        for h in range(H):
            for vt in range(VT):
                block = acc[h * JW : (h + 1) * JW, vt * PV : (vt + 1) * PV]
                part[h, c, vt * JT : (vt + 1) * JT] = block.reshape(JT, JT_ROWS, PV)

    def swap(h, c):
        return pltpu.make_async_remote_copy(
            src_ref=part.at[h, c, pl.ds((1 - side) * half, half)],
            dst_ref=paired.at[h, c],
            send_sem=swap_s.at[h, c],
            recv_sem=swap_r.at[h, c],
            device_id={"ov": twin},
            device_id_type=MESH,
        )

    def scatter(h, c, step):
        return pltpu.make_async_remote_copy(
            src_ref=halves.at[h, c, lax.rem(group + step, half)],
            dst_ref=arrived.at[h, c, step],
            send_sem=scat_s.at[h, c, step],
            recv_sem=scat_r.at[h, c, step],
            device_id={"ov": mate(step)},
            device_id_type=MESH,
        )

    def gather(h, c, step, at_piece):
        return pltpu.make_async_remote_copy(
            src_ref=coup.at[h, c, side * half + at_piece],
            dst_ref=coup.at[h, c, side * half + at_piece],
            send_sem=gath_s.at[h, c, step],
            recv_sem=gath_r.at[h, c, step],
            device_id={"ov": mate(step)},
            device_id_type=MESH,
        )

    def onward(h, c, step, hand):
        return pltpu.make_async_remote_copy(
            src_ref=coup.at[h, c, hand * half + origin(step)],
            dst_ref=coup.at[h, c, hand * half + origin(step)],
            send_sem=on_s.at[h, c, step],
            recv_sem=on_r.at[h, c, step],
            device_id={"ov": twin},
            device_id_type=MESH,
        )

    def step1(h, c):
        swap(h, c).start()

    def step2(h, c):
        swap(h, c).wait_recv()

        @pl.loop(1, half)
        def _(step):
            piece = lax.rem(group + step, half)
            halves[h, c, piece] = (part[h, c, side * half + piece] + paired[h, c, piece]).astype(halves.dtype)
            scatter(h, c, step).start()

        own[h, c] = part[h, c, side * half + group] + paired[h, c, group]

    def step3(h, c):
        @pl.loop(1, half)
        def _(step):
            scatter(h, c, step).wait_recv()
            own[h, c] += arrived[h, c, step].astype(jnp.float32)

        coup[h, c, side * half + group] = own[h, c].astype(coup.dtype)

        @pl.loop(1, half)
        def _(step):
            gather(h, c, step, group).start()

        onward(h, c, 0, side).start()

    def step4(h, c):
        @pl.loop(1, half)
        def _(step):
            gather(h, c, step, origin(step)).wait_recv()
            onward(h, c, step, side).start()

    def step5(h, c):
        @pl.loop(0, half)
        def _(step):
            onward(h, c, step, 1 - side).wait_recv()

        for vt in range(VT):
            block = coup[h, c, vt * JT : (vt + 1) * JT].reshape(JW, PV)
            weights[h, c * VC + vt * PV : c * VC + (vt + 1) * PV, :] = block.T

    early, late = NB // 2, (3 * NB) // 4
    for c in range(NC):
        acc[...] = jnp.zeros_like(acc)
        compute(c, 0, early)
        if c >= 1:
            step2(0, c - 1)
        compute(c, early, late)
        if c >= 2:
            step3(0, c - 2)
        compute(c, late, NB)
        if c >= 3:
            step4(0, c - 3)
        store_part(c)
        if c == 0:
            pl.semaphore_wait(barrier, half + groups - 1)
        step1(0, c)

    for q in range(min(TILE_RING, jobs)):
        t_copy(jnp.int32(q)).start()
    p_copy = pltpu.make_async_copy(prior, pbuf, p_sem)
    p_copy.start()

    late_steps = []
    for c in range(NC):
        if c >= NC - 1:
            late_steps.append((1, step2, c))
        if c >= NC - 2:
            late_steps.append((2 + 2 * (c - NC + 2), step3, c))
        if c >= NC - 3:
            late_steps.append((3 + 2 * (c - NC + 2), step4, c))
    for _, run, c in sorted(late_steps, key=lambda item: item[0]):
        run(0, c)
    for c in range(NC):
        step5(0, c)

    def x_copy(h, d, t, target):
        return pltpu.make_async_remote_copy(
            src_ref=sbuf.at[h, d - 1, t],
            dst_ref=rbuf.at[h, d - 1, t],
            send_sem=x_s.at[h, d - 1, t],
            recv_sem=x_r.at[h, d - 1, t],
            device_id={"vec": target},
            device_id_type=MESH,
        )

    def tile_product(h, q):
        t_copy(q).wait()
        product = jnp.dot(
            tiles[lax.rem(q, TILE_RING)], weights[h], preferred_element_type=jnp.float32
        )
        return product

    def refill(q):
        @pl.when(q + TILE_RING < jobs)
        def _():
            t_copy(q + TILE_RING).start()

    def share_tiles(h, first, last):
        @pl.loop(first, last)
        def _(t):
            for d in range(1, groups):
                q = h * shares + t * (groups - 1) + d - 1
                sbuf[h, d - 1, t] = tile_product(h, q).astype(sbuf.dtype)
                x_copy(h, d, t, lax.rem(vec + d, groups)).start()
                refill(q)

    def final_tiles(h):
        @pl.loop(0, NT)
        def _(t):
            q = H * shares + h * NT + t
            total_tile = tile_product(h, q)
            refill(q)
            rows = pl.ds(pl.multiple_of(t * TR, TR), TR)
            columns = slice(h * JW, (h + 1) * JW)
            for d in range(1, groups):
                x_copy(h, d, t, lax.rem(vec + d, groups)).wait_recv()
                total_tile += rbuf[h, d - 1, t].astype(jnp.float32)
            out[rows, columns] = (pbuf[rows, columns].astype(jnp.float32) + total_tile).astype(out.dtype)

    for h in range(H):
        if h + 1 < H:
            for c in range(NC):
                step1(h + 1, c)
            edges = [0, NT // 8, NT // 2, (3 * NT) // 4, NT]
            for k, run in enumerate((step2, step3, step4, step5)):
                share_tiles(h, edges[k], edges[k + 1])
                for c in range(NC):
                    run(h + 1, c)
        else:
            share_tiles(h, 0, NT)
    p_copy.wait()
    for h in range(H):
        final_tiles(h)

    for h in range(H):
        for c in range(NC):
            swap(h, c).wait_send()

            @pl.loop(1, half)
            def _(step):
                scatter(h, c, step).wait_send()
                gather(h, c, step, group).wait_send()

            @pl.loop(0, half)
            def _(step):
                onward(h, c, step, side).wait_send()

        for d in range(1, groups):

            @pl.loop(0, NT)
            def _(t):
                x_copy(h, d, t, lax.rem(vec + d, groups)).wait_send()


def body(n, groups, chol, amplitudes, prior):
    rows, vectors = chol.shape
    columns = amplitudes.shape[1]
    half = n // 2
    VC = divisor(vectors, (CHUNK, 256, 128))
    H = 2 if VC * (columns // 2) // JT_ROWS // n >= 128 else 1
    NC = vectors // VC
    RB = halved(rows, 2048)
    NB = rows // RB
    JW = columns // H
    PV = VC * (JW // JT_ROWS) // n
    TR = divisor(prior.shape[0], (256, 128, 64, 32, 16))
    NT = prior.shape[0] // TR
    plan = (n, groups, H, NC, NB, RB, VC, PV, JW, TR, NT)
    bf16, f32 = jnp.bfloat16, jnp.float32
    dma = pltpu.SemaphoreType.DMA
    return pl.pallas_call(
        functools.partial(kernel, plan),
        out_shape=jax.ShapeDtypeStruct(prior.shape, prior.dtype),
        in_specs=[pl.BlockSpec(memory_space=pl.ANY)] * 3,
        out_specs=pl.BlockSpec(memory_space=pltpu.VMEM),
        scratch_shapes=[
            pltpu.VMEM((NB, RB, columns), bf16),
            pltpu.VMEM((NB, columns, RB), bf16),
            pltpu.VMEM((RING, RB, VC), bf16),
            pltpu.VMEM((columns, VC), f32),
            pltpu.VMEM((H, NC, n, JT_ROWS, PV), f32),
            pltpu.VMEM((H, NC, half, JT_ROWS, PV), f32),
            pltpu.VMEM((H, NC, half, JT_ROWS, PV), bf16),
            pltpu.VMEM((H, NC, half, JT_ROWS, PV), bf16),
            pltpu.VMEM((H, NC, JT_ROWS, PV), f32),
            pltpu.VMEM((H, NC, n, JT_ROWS, PV), bf16),
            pltpu.VMEM((H, vectors, JW), bf16),
            pltpu.VMEM((TILE_RING, TR, vectors), bf16),
            pltpu.VMEM((H, groups - 1, NT, TR, JW), bf16),
            pltpu.VMEM((H, groups - 1, NT, TR, JW), bf16),
            pltpu.VMEM(prior.shape, bf16),
            dma((NB,)),
            dma((RING,)),
            dma((TILE_RING,)),
            dma(()),
            dma((H, NC)),
            dma((H, NC)),
        ]
        + [dma((H, NC, half))] * 6
        + [dma((H, groups - 1, NT))] * 2,
        compiler_params=pltpu.CompilerParams(
            collective_id=0, has_side_effects=True, vmem_limit_bytes=61 * 2**20
        ),
    )(chol, amplitudes, prior)


def solution(mesh):
    return jax.shard_map(
        functools.partial(body, mesh.shape["ov"], mesh.shape["vec"]),
        mesh=mesh,
        in_specs=(P("ov", "vec"), P("ov", None), P(("ov", "vec"), None)),
        out_specs=P(("ov", "vec"), None),
        check_vma=False,
    )
```

profile of v0, /device:TPU:0, one launch (start us, length us, event | category | flops | bytes accessed | tf_op | source)
XLA Modules:
  0.0 121.5 jit_solution(17613439945730433702)
XLA Ops:
  0.0 117.7 %shard_map.37 = bf16[6144,256]{1,0:T(8,128)(2,1)} custom-call(bf16[12288,2048]{1,0:T(8,128)(2,1)} %chol.1, bf16[12288,256]{1,0:T(8,128)(2,1)} %amplitudes.1, bf16[6144,256]{1,0:T(8,128)(2,1)} %prior.1), custom_call_target="tpu_custom_call" | custom-call | tf_op jit(solution)/shard_map/pallas_call | solution.py:335
  117.7 3.8 %copy.5 = bf16[6144,256]{1,0:T(8,128)(2,1)} copy(bf16[6144,256]{1,0:T(8,128)(2,1)} %shard_map.37) | data formatting | bytes 6291456
where the time goes:
time: 122 us
  Pallas kernels  118 us (97%)
  local copies, waits for them, and re-layouts  3.76 us (3%)
    pallas_call x1, Pallas kernels, body(): pl.pallas_call(functools.partial(kernel, plan), out_shape=jax.ShapeDtypeS...  118 us
    unnamed x1, local copies, waits for them, and re-layouts  3.76 us

commit v1 on v0

--- a/solution.py
+++ b/solution.py
@@ -10,7 +10,7 @@
 MESH = pl.DeviceIdType.MESH
 JT_ROWS = 16
 CHUNK = 512
-RING = 6
+RING = 3
 TILE_RING = 6
 
 
@@ -119,45 +119,34 @@
                 block = acc[h * JW : (h + 1) * JW, vt * PV : (vt + 1) * PV]
                 part[h, c, vt * JT : (vt + 1) * JT] = block.reshape(JT, JT_ROWS, PV)
 
+    def to_ov(src, dst, send_sem, recv_sem, device):
+        return pltpu.make_async_remote_copy(
+            src_ref=src, dst_ref=dst, send_sem=send_sem, recv_sem=recv_sem,
+            device_id={"ov": device}, device_id_type=MESH,
+        )
+
     def swap(h, c):
-        return pltpu.make_async_remote_copy(
-            src_ref=part.at[h, c, pl.ds((1 - side) * half, half)],
-            dst_ref=paired.at[h, c],
-            send_sem=swap_s.at[h, c],
-            recv_sem=swap_r.at[h, c],
-            device_id={"ov": twin},
-            device_id_type=MESH,
-        )
+        there = part.at[h, c, pl.ds((1 - side) * half, half)]
+        return to_ov(there, paired.at[h, c], swap_s, swap_r.at[h, c], twin)
 
     def scatter(h, c, step):
-        return pltpu.make_async_remote_copy(
-            src_ref=halves.at[h, c, lax.rem(group + step, half)],
-            dst_ref=arrived.at[h, c, step],
-            send_sem=scat_s.at[h, c, step],
-            recv_sem=scat_r.at[h, c, step],
-            device_id={"ov": mate(step)},
-            device_id_type=MESH,
-        )
-
-    def gather(h, c, step, at_piece):
-        return pltpu.make_async_remote_copy(
-            src_ref=coup.at[h, c, side * half + at_piece],
-            dst_ref=coup.at[h, c, side * half + at_piece],
-            send_sem=gath_s.at[h, c, step],
-            recv_sem=gath_r.at[h, c, step],
-            device_id={"ov": mate(step)},
-            device_id_type=MESH,
-        )
-
-    def onward(h, c, step, hand):
-        return pltpu.make_async_remote_copy(
-            src_ref=coup.at[h, c, hand * half + origin(step)],
-            dst_ref=coup.at[h, c, hand * half + origin(step)],
-            send_sem=on_s.at[h, c, step],
-            recv_sem=on_r.at[h, c, step],
-            device_id={"ov": twin},
-            device_id_type=MESH,
-        )
+        piece = halves.at[h, c, lax.rem(group + step, half)]
+        return to_ov(piece, arrived.at[h, c, step - 1], scat_s, scat_r.at[h, c], mate(step))
+
+    def gather(h, c, step):
+        piece = coup.at[h, c, side * half + group]
+        return to_ov(piece, piece, gath_s, gath_r.at[h, c], mate(step))
+
+    def onward(h, c, hand):
+        pieces = coup.at[h, c, pl.ds(hand * half, half)]
+        return to_ov(pieces, pieces, on_s, on_r.at[h, c], twin)
+
+    def all_scattered(h, c):
+        return to_ov(arrived.at[h, c], arrived.at[h, c], scat_s, scat_r.at[h, c], twin)
+
+    def all_gathered(h, c):
+        pieces = coup.at[h, c, pl.ds(side * half, half - 1)]
+        return to_ov(pieces, pieces, gath_s, gath_r.at[h, c], twin)
 
     def step1(h, c):
         swap(h, c).start()
@@ -174,30 +163,22 @@
         own[h, c] = part[h, c, side * half + group] + paired[h, c, group]
 
     def step3(h, c):
+        all_scattered(h, c).wait_recv()
+        total = own[h, c]
+        for step in range(1, half):
+            total += arrived[h, c, step - 1].astype(jnp.float32)
+        coup[h, c, side * half + group] = total.astype(coup.dtype)
+
         @pl.loop(1, half)
         def _(step):
-            scatter(h, c, step).wait_recv()
-            own[h, c] += arrived[h, c, step].astype(jnp.float32)
-
-        coup[h, c, side * half + group] = own[h, c].astype(coup.dtype)
-
-        @pl.loop(1, half)
-        def _(step):
-            gather(h, c, step, group).start()
-
-        onward(h, c, 0, side).start()
+            gather(h, c, step).start()
 
     def step4(h, c):
-        @pl.loop(1, half)
-        def _(step):
-            gather(h, c, step, origin(step)).wait_recv()
-            onward(h, c, step, side).start()
+        all_gathered(h, c).wait_recv()
+        onward(h, c, side).start()
 
     def step5(h, c):
-        @pl.loop(0, half)
-        def _(step):
-            onward(h, c, step, 1 - side).wait_recv()
-
+        onward(h, c, 1 - side).wait_recv()
         for vt in range(VT):
             block = coup[h, c, vt * JT : (vt + 1) * JT].reshape(JW, PV)
             weights[h, c * VC + vt * PV : c * VC + (vt + 1) * PV, :] = block.T
@@ -224,24 +205,25 @@
     p_copy = pltpu.make_async_copy(prior, pbuf, p_sem)
     p_copy.start()
 
-    late_steps = []
-    for c in range(NC):
-        if c >= NC - 1:
-            late_steps.append((1, step2, c))
-        if c >= NC - 2:
-            late_steps.append((2 + 2 * (c - NC + 2), step3, c))
-        if c >= NC - 3:
-            late_steps.append((3 + 2 * (c - NC + 2), step4, c))
-    for _, run, c in sorted(late_steps, key=lambda item: item[0]):
-        run(0, c)
-    for c in range(NC):
+    step2(0, NC - 1)
+    if NC >= 2:
+        step3(0, NC - 2)
+    if NC >= 3:
+        step4(0, NC - 3)
+    for c in range(NC - 2):
         step5(0, c)
+    step3(0, NC - 1)
+    if NC >= 2:
+        step4(0, NC - 2)
+        step5(0, NC - 2)
+    step4(0, NC - 1)
+    step5(0, NC - 1)
 
     def x_copy(h, d, t, target):
         return pltpu.make_async_remote_copy(
             src_ref=sbuf.at[h, d - 1, t],
             dst_ref=rbuf.at[h, d - 1, t],
-            send_sem=x_s.at[h, d - 1, t],
+            send_sem=x_s,
             recv_sem=x_r.at[h, d - 1, t],
             device_id={"vec": target},
             device_id_type=MESH,
@@ -296,24 +278,11 @@
     for h in range(H):
         final_tiles(h)
 
-    for h in range(H):
-        for c in range(NC):
-            swap(h, c).wait_send()
-
-            @pl.loop(1, half)
-            def _(step):
-                scatter(h, c, step).wait_send()
-                gather(h, c, step, group).wait_send()
-
-            @pl.loop(0, half)
-            def _(step):
-                onward(h, c, step, side).wait_send()
-
-        for d in range(1, groups):
-
-            @pl.loop(0, NT)
-            def _(t):
-                x_copy(h, d, t, lax.rem(vec + d, groups)).wait_send()
+    to_ov(paired, paired, swap_s, swap_r.at[0, 0], twin).wait_send()
+    to_ov(arrived, arrived, scat_s, scat_r.at[0, 0], twin).wait_send()
+    to_ov(arrived, arrived, gath_s, gath_r.at[0, 0], twin).wait_send()
+    to_ov(halves, halves, on_s, on_r.at[0, 0], twin).wait_send()
+    to_ov(sbuf, sbuf, x_s, x_r.at[0, 0, 0], twin).wait_send()
 
 
 def body(n, groups, chol, amplitudes, prior):
@@ -323,7 +292,7 @@
     VC = divisor(vectors, (CHUNK, 256, 128))
     H = 2 if VC * (columns // 2) // JT_ROWS // n >= 128 else 1
     NC = vectors // VC
-    RB = halved(rows, 2048)
+    RB = halved(rows, 4096)
     NB = rows // RB
     JW = columns // H
     PV = VC * (JW // JT_ROWS) // n
@@ -334,7 +303,7 @@
     dma = pltpu.SemaphoreType.DMA
     return pl.pallas_call(
         functools.partial(kernel, plan),
-        out_shape=jax.ShapeDtypeStruct(prior.shape, prior.dtype),
+        out_shape=pltpu.VMEM(prior.shape, prior.dtype),
         in_specs=[pl.BlockSpec(memory_space=pl.ANY)] * 3,
         out_specs=pl.BlockSpec(memory_space=pltpu.VMEM),
         scratch_shapes=[
@@ -345,7 +314,7 @@
             pltpu.VMEM((H, NC, n, JT_ROWS, PV), f32),
             pltpu.VMEM((H, NC, half, JT_ROWS, PV), f32),
             pltpu.VMEM((H, NC, half, JT_ROWS, PV), bf16),
-            pltpu.VMEM((H, NC, half, JT_ROWS, PV), bf16),
+            pltpu.VMEM((H, NC, half - 1, JT_ROWS, PV), bf16),
             pltpu.VMEM((H, NC, JT_ROWS, PV), f32),
             pltpu.VMEM((H, NC, n, JT_ROWS, PV), bf16),
             pltpu.VMEM((H, vectors, JW), bf16),
@@ -357,13 +326,19 @@
             dma((RING,)),
             dma((TILE_RING,)),
             dma(()),
+            dma(()),
             dma((H, NC)),
+            dma(()),
             dma((H, NC)),
-        ]
-        + [dma((H, NC, half))] * 6
-        + [dma((H, groups - 1, NT))] * 2,
+            dma(()),
+            dma((H, NC)),
+            dma(()),
+            dma((H, NC)),
+            dma(()),
+            dma((H, groups - 1, NT)),
+        ],
         compiler_params=pltpu.CompilerParams(
-            collective_id=0, has_side_effects=True, vmem_limit_bytes=61 * 2**20
+            collective_id=0, has_side_effects=True, vmem_limit_bytes=54 * 2**20
         ),
     )(chol, amplitudes, prior)
 

time: 122 us -> 106 us (0.87)
  Pallas kernels: 118 us -> 104 us
  local copies, waits for them, and re-layouts: 3.76 us -> 1.67 us
    pallas_call x1, Pallas kernels: 118 us -> 104 us  [body(): pl.pallas_call(functools.partial(kernel, plan), out_shape=pltpu.VMEM(prio...]
    unnamed x1, local copies, waits for them, and re-layouts: 3.76 us -> 1.67 us
where the time goes in v1:
time: 106 us; the launch traced here: 105 us
  Pallas kernels  104 us (98%)
  local copies, waits for them, and re-layouts  1.67 us (2%)
    pallas_call x1, Pallas kernels, body(): pl.pallas_call(functools.partial(kernel, plan), out_shape=pltpu.VMEM(prio...  104 us

profile of v1, /device:TPU:0, one launch (start us, length us, event | category | flops | bytes accessed | tf_op | source)
XLA Modules:
  0.0 105.4 jit_solution(16040406060246156703)
XLA Ops:
  0.0 103.7 %shard_map.37 = bf16[6144,256]{1,0:T(8,128)(2,1)S(1)} custom-call(bf16[12288,2048]{1,0:T(8,128)(2,1)} %chol.1, bf16[12288,256]{1,0:T(8,128)(2,1)} %amplitudes.1, bf16[6144,256]{1,0:T(8,128)(2,1)} %prior.1), custom_call_target="tpu_custom_call" | custom-call | tf_op jit(solution)/shard_map/pallas_call | solution.py:304
  103.7 1.7 %copy.5 = bf16[6144,256]{1,0:T(8,128)(2,1)} copy(bf16[6144,256]{1,0:T(8,128)(2,1)S(1)} %shard_map.37) | data formatting | bytes 6291456

commit v2 on v1

--- a/solution.py
+++ b/solution.py
@@ -29,10 +29,11 @@
 
 def kernel(
     plan, chol, amplitudes, prior, out,
-    abuf, at, lbuf, acc, part, paired, halves, arrived, own, coup, weights, tiles, sbuf, rbuf, pbuf,
+    abuf, at, lbuf, acc, part, paired, halves, arrived, own, coup, weights, tiles, sbuf, rbuf, pbuf, raw, coup2, weights2,
     a_sems, l_sems, t_sems, p_sem, swap_s, swap_r, scat_s, scat_r, gath_s, gath_r, on_s, on_r, x_s, x_r,
+    raw_s, raw_r, cross_s, cross_r, gath2_s, gath2_r, on2_s, on2_r,
 ):
-    n, groups, H, NC, NB, RB, VC, PV, JW, TR, NT = plan
+    n, groups, H, NC, NB, RB, VC, PV, JW, TR, NT, NS = plan
     half = n // 2
     me = lax.axis_index("ov")
     vec = lax.axis_index("vec")
@@ -63,13 +64,18 @@
         )
 
     total = NC * NB
-    shares = NT * (groups - 1)
+    shares = NS * (groups - 1)
     jobs = H * (shares + NT)
+    early_rows = NS < NT
+
+    def final_tile_of(h, i):
+        return jnp.where(h > 0, lax.rem(i + NS, NT), i)
 
     def job_row(q):
         final = q >= H * shares
         k = lax.rem(q, shares)
-        t = jnp.where(final, lax.rem(q - H * shares, NT), k // (groups - 1))
+        i = q - H * shares
+        t = jnp.where(final, final_tile_of(i // NT, lax.rem(i, NT)), k // (groups - 1))
         d = jnp.where(final, 0, lax.rem(k, groups - 1) + 1)
         return lax.rem(vec + d, groups) * rows_out + t * TR
 
@@ -168,6 +174,8 @@
         for step in range(1, half):
             total += arrived[h, c, step - 1].astype(jnp.float32)
         coup[h, c, side * half + group] = total.astype(coup.dtype)
+        if early_rows:
+            cross(h, c).start()
 
         @pl.loop(1, half)
         def _(step):
@@ -182,6 +190,50 @@
         for vt in range(VT):
             block = coup[h, c, vt * JT : (vt + 1) * JT].reshape(JW, PV)
             weights[h, c * VC + vt * PV : c * VC + (vt + 1) * PV, :] = block.T
+
+    other = lax.rem(vec + 1, groups)
+    def raw_copy():
+        return pltpu.make_async_remote_copy(
+            src_ref=chol.at[pl.ds(pl.multiple_of(other * rows_out + (NT - 1) * TR, TR), TR), :],
+            dst_ref=raw,
+            send_sem=raw_s,
+            recv_sem=raw_r,
+            device_id={"vec": other},
+            device_id_type=MESH,
+        )
+
+    def cross(h, c):
+        return pltpu.make_async_remote_copy(
+            src_ref=coup.at[h, c, side * half + group],
+            dst_ref=coup2.at[h, c, side * half + group],
+            send_sem=cross_s.at[h, c],
+            recv_sem=cross_r.at[h, c],
+            device_id={"vec": other},
+            device_id_type=MESH,
+        )
+
+    def step6(h, c):
+        cross(h, c).wait_recv()
+
+        @pl.loop(1, half)
+        def _(step):
+            piece = coup2.at[h, c, side * half + group]
+            to_ov(piece, piece, gath2_s, gath2_r.at[h, c], mate(step)).start()
+
+    def onward2(h, c, hand):
+        pieces = coup2.at[h, c, pl.ds(hand * half, half)]
+        return to_ov(pieces, pieces, on2_s, on2_r.at[h, c], twin)
+
+    def step7(h, c):
+        pieces = coup2.at[h, c, pl.ds(side * half, half - 1)]
+        to_ov(pieces, pieces, gath2_s, gath2_r.at[h, c], twin).wait_recv()
+        onward2(h, c, side).start()
+
+    def step8(h, c):
+        onward2(h, c, 1 - side).wait_recv()
+        for vt in range(VT):
+            block = coup2[h, c, vt * JT : (vt + 1) * JT].reshape(JW, PV)
+            weights2[h, c * VC + vt * PV : c * VC + (vt + 1) * PV, :] = block.T
 
     early, late = NB // 2, (3 * NB) // 4
     for c in range(NC):
@@ -198,6 +250,8 @@
         store_part(c)
         if c == 0:
             pl.semaphore_wait(barrier, half + groups - 1)
+            if early_rows:
+                raw_copy().start()
         step1(0, c)
 
     for q in range(min(TILE_RING, jobs)):
@@ -250,39 +304,68 @@
                 x_copy(h, d, t, lax.rem(vec + d, groups)).start()
                 refill(q)
 
-    def final_tiles(h):
-        @pl.loop(0, NT)
-        def _(t):
-            q = H * shares + h * NT + t
-            total_tile = tile_product(h, q)
-            refill(q)
-            rows = pl.ds(pl.multiple_of(t * TR, TR), TR)
-            columns = slice(h * JW, (h + 1) * JW)
+    def final_tile(h, i, with_raw):
+        q = H * shares + h * NT + i
+        t = final_tile_of(h, i)
+        total_tile = tile_product(h, q)
+        refill(q)
+        rows = pl.ds(pl.multiple_of(t * TR, TR), TR)
+        columns = slice(h * JW, (h + 1) * JW)
+        if with_raw:
+            total_tile += jnp.dot(raw[...], weights2[h], preferred_element_type=jnp.float32)
+        else:
             for d in range(1, groups):
                 x_copy(h, d, t, lax.rem(vec + d, groups)).wait_recv()
                 total_tile += rbuf[h, d - 1, t].astype(jnp.float32)
-            out[rows, columns] = (pbuf[rows, columns].astype(jnp.float32) + total_tile).astype(out.dtype)
+        out[rows, columns] = (pbuf[rows, columns].astype(jnp.float32) + total_tile).astype(out.dtype)
+
+    def final_tiles(h, first, last):
+        @pl.loop(first, last)
+        def _(i):
+            final_tile(h, i, False)
 
     for h in range(H):
         if h + 1 < H:
             for c in range(NC):
                 step1(h + 1, c)
-            edges = [0, NT // 8, NT // 2, (3 * NT) // 4, NT]
+            edges = [0, NS // 8, NS // 2, (3 * NS) // 4, NS]
             for k, run in enumerate((step2, step3, step4, step5)):
                 share_tiles(h, edges[k], edges[k + 1])
                 for c in range(NC):
                     run(h + 1, c)
         else:
-            share_tiles(h, 0, NT)
+            share_tiles(h, 0, NS)
     p_copy.wait()
-    for h in range(H):
-        final_tiles(h)
+    every = [(h, c) for h in range(H) for c in range(NC)]
+    if early_rows:
+        for h, c in every:
+            step6(h, c)
+        final_tiles(0, 0, NT // 2)
+        for h, c in every:
+            step7(h, c)
+        final_tiles(0, NT // 2, NS)
+        for h, c in every:
+            step8(h, c)
+        raw_copy().wait_recv()
+        final_tile(0, jnp.int32(NS), True)
+        for h in range(1, H):
+            final_tile(h, jnp.int32(0), True)
+            final_tiles(h, 1, NT)
+    else:
+        for h in range(H):
+            final_tiles(h, 0, NT)
 
     to_ov(paired, paired, swap_s, swap_r.at[0, 0], twin).wait_send()
     to_ov(arrived, arrived, scat_s, scat_r.at[0, 0], twin).wait_send()
     to_ov(arrived, arrived, gath_s, gath_r.at[0, 0], twin).wait_send()
     to_ov(halves, halves, on_s, on_r.at[0, 0], twin).wait_send()
     to_ov(sbuf, sbuf, x_s, x_r.at[0, 0, 0], twin).wait_send()
+    if early_rows:
+        raw_copy().wait_send()
+        for h, c in every:
+            cross(h, c).wait_send()
+        to_ov(arrived, arrived, gath2_s, gath2_r.at[0, 0], twin).wait_send()
+        to_ov(halves, halves, on2_s, on2_r.at[0, 0], twin).wait_send()
 
 
 def body(n, groups, chol, amplitudes, prior):
@@ -298,7 +381,8 @@
     PV = VC * (JW // JT_ROWS) // n
     TR = divisor(prior.shape[0], (256, 128, 64, 32, 16))
     NT = prior.shape[0] // TR
-    plan = (n, groups, H, NC, NB, RB, VC, PV, JW, TR, NT)
+    NS = NT - 1 if groups == 2 and NT > 2 else NT
+    plan = (n, groups, H, NC, NB, RB, VC, PV, JW, TR, NT, NS)
     bf16, f32 = jnp.bfloat16, jnp.float32
     dma = pltpu.SemaphoreType.DMA
     return pl.pallas_call(
@@ -319,9 +403,12 @@
             pltpu.VMEM((H, NC, n, JT_ROWS, PV), bf16),
             pltpu.VMEM((H, vectors, JW), bf16),
             pltpu.VMEM((TILE_RING, TR, vectors), bf16),
-            pltpu.VMEM((H, groups - 1, NT, TR, JW), bf16),
-            pltpu.VMEM((H, groups - 1, NT, TR, JW), bf16),
+            pltpu.VMEM((H, groups - 1, NS, TR, JW), bf16),
+            pltpu.VMEM((H, groups - 1, NS, TR, JW), bf16),
             pltpu.VMEM(prior.shape, bf16),
+            pltpu.VMEM((TR, vectors), bf16),
+            pltpu.VMEM((H, NC, n, JT_ROWS, PV), bf16),
+            pltpu.VMEM((H, vectors, JW), bf16),
             dma((NB,)),
             dma((RING,)),
             dma((TILE_RING,)),
@@ -335,7 +422,15 @@
             dma(()),
             dma((H, NC)),
             dma(()),
-            dma((H, groups - 1, NT)),
+            dma((H, groups - 1, NS)),
+            dma(()),
+            dma(()),
+            dma((H, NC)),
+            dma((H, NC)),
+            dma(()),
+            dma((H, NC)),
+            dma(()),
+            dma((H, NC)),
         ],
         compiler_params=pltpu.CompilerParams(
             collective_id=0, has_side_effects=True, vmem_limit_bytes=54 * 2**20

time: 106 us -> 104 us (0.981)
  Pallas kernels: 104 us -> 102 us
    pallas_call x1, Pallas kernels: 104 us -> 102 us  [body(): pl.pallas_call(functools.partial(kernel, plan), out_shape=pltpu.VMEM(prio...]
where the time goes in v2:
time: 104 us
  Pallas kernels  102 us (98%)
  local copies, waits for them, and re-layouts  1.67 us (2%)
    pallas_call x1, Pallas kernels, body(): pl.pallas_call(functools.partial(kernel, plan), out_shape=pltpu.VMEM(prio...  102 us

profile of v2, /device:TPU:0, one launch (start us, length us, event | category | flops | bytes accessed | tf_op | source)
XLA Modules:
  0.0 104.0 jit_solution(12093772647107364363)
XLA Ops:
  0.0 102.3 %shard_map.37 = bf16[6144,256]{1,0:T(8,128)(2,1)S(1)} custom-call(bf16[12288,2048]{1,0:T(8,128)(2,1)} %chol.1, bf16[12288,256]{1,0:T(8,128)(2,1)} %amplitudes.1, bf16[6144,256]{1,0:T(8,128)(2,1)} %prior.1), custom_call_target="tpu_custom_call" | custom-call | tf_op jit(solution)/shard_map/pallas_call | solution.py:388
  102.3 1.7 %copy.5 = bf16[6144,256]{1,0:T(8,128)(2,1)} copy(bf16[6144,256]{1,0:T(8,128)(2,1)S(1)} %shard_map.37) | data formatting | bytes 6291456

commit v3 on v2

--- a/solution.py
+++ b/solution.py
@@ -174,12 +174,13 @@
         for step in range(1, half):
             total += arrived[h, c, step - 1].astype(jnp.float32)
         coup[h, c, side * half + group] = total.astype(coup.dtype)
-        if early_rows:
-            cross(h, c).start()
 
         @pl.loop(1, half)
         def _(step):
             gather(h, c, step).start()
+
+        if early_rows:
+            cross(h, c).start()
 
     def step4(h, c):
         all_gathered(h, c).wait_recv()
@@ -271,6 +272,13 @@
         step4(0, NC - 2)
         step5(0, NC - 2)
     step4(0, NC - 1)
+    known = (NC - 1) * VC
+    ahead = NC > 1 and NS // 8 > 1 and H > 1 and groups == 2 and TR <= acc.shape[0]
+    if ahead:
+        t_copy(jnp.int32(0)).wait()
+        acc[:TR, :JW] = jnp.dot(
+            tiles[0, :, :known], weights[0, :known], preferred_element_type=jnp.float32
+        )
     step5(0, NC - 1)
 
     def x_copy(h, d, t, target):
@@ -294,6 +302,12 @@
         @pl.when(q + TILE_RING < jobs)
         def _():
             t_copy(q + TILE_RING).start()
+
+    def first_share():
+        rest = jnp.dot(tiles[0, :, known:], weights[0, known:], preferred_element_type=jnp.float32)
+        sbuf[0, 0, 0] = (acc[:TR, :JW] + rest).astype(sbuf.dtype)
+        x_copy(0, 1, 0, lax.rem(vec + 1, groups)).start()
+        refill(jnp.int32(0))
 
     def share_tiles(h, first, last):
         @pl.loop(first, last)
@@ -324,11 +338,13 @@
         def _(i):
             final_tile(h, i, False)
 
+    if ahead:
+        first_share()
     for h in range(H):
         if h + 1 < H:
             for c in range(NC):
                 step1(h + 1, c)
-            edges = [0, NS // 8, NS // 2, (3 * NS) // 4, NS]
+            edges = [1 if h == 0 and ahead else 0, NS // 8, NS // 2, (3 * NS) // 4, NS]
             for k, run in enumerate((step2, step3, step4, step5)):
                 share_tiles(h, edges[k], edges[k + 1])
                 for c in range(NC):

time: 104 us -> 104 us (level)
  no operation moved by 1% of the time
where the time goes in v3:
time: 104 us
  Pallas kernels  103 us (99%)
  local copies, waits for them, and re-layouts  1.67 us (2%)
    pallas_call x1, Pallas kernels, body(): pl.pallas_call(functools.partial(kernel, plan), out_shape=pltpu.VMEM(prio...  103 us

profile of v3, /device:TPU:0, one launch (start us, length us, event | category | flops | bytes accessed | tf_op | source)
XLA Modules:
  0.0 104.2 jit_solution(7753125624086607696)
XLA Ops:
  0.0 102.5 %shard_map.37 = bf16[6144,256]{1,0:T(8,128)(2,1)S(1)} custom-call(bf16[12288,2048]{1,0:T(8,128)(2,1)} %chol.1, bf16[12288,256]{1,0:T(8,128)(2,1)} %amplitudes.1, bf16[6144,256]{1,0:T(8,128)(2,1)} %prior.1), custom_call_target="tpu_custom_call" | custom-call | tf_op jit(solution)/shard_map/pallas_call | solution.py:404
  102.5 1.7 %copy.5 = bf16[6144,256]{1,0:T(8,128)(2,1)} copy(bf16[6144,256]{1,0:T(8,128)(2,1)S(1)} %shard_map.37) | data formatting | bytes 6291456
